TPU v7x, 32 devices: a whole 2x2x4 slice. The times are simulated.
32 devices in a mesh: ep: 4 (over z), fsdp: 4 (over x, core), tp: 2 (over y).
Axes of the slice: x: 2, y: 2, z: 4, core: 2. Of those that a mesh axis runs over, the one named last changes fastest.
Arguments:
- out_grad: bfloat16 [2048, 4096], P(('ep', 'fsdp')), may hold values from -1.5 to 1.5
- routes: int32 [2048, 2], P(('ep', 'fsdp')), may hold values from 0 to 3, all different within a row; in each aligned block of 128 rows (0 to 127, 128 to 255, ...) at most 128 rows name the same one
- chosen_logits: float32 [2048, 2], P(('ep', 'fsdp')), may hold values from -4 to 4
- routed_inputs: bfloat16 [4, 4, 4, 128, 4096], P('ep', None, 'fsdp'), may hold values from -6 to 6
- w_gate: bfloat16 [4, 4096, 512], P('ep', 'fsdp', 'tp'), may hold values from -0.09375 to 0.09375
- w_up: bfloat16 [4, 4096, 512], P('ep', 'fsdp', 'tp'), may hold values from -0.09375 to 0.09375
- w_down: bfloat16 [4, 512, 4096], P('ep', 'tp', 'fsdp'), may hold values from -0.25 to 0.25
Outputs:
- input_grad: bfloat16 [2048, 4096], P(('ep', 'fsdp'))
- logit_grad: float32 [2048, 2], P(('ep', 'fsdp'))
- grad_gate: float32 [4, 4096, 512], P('ep', 'fsdp', 'tp')
- grad_up: float32 [4, 4096, 512], P('ep', 'fsdp', 'tp')
- grad_down: float32 [4, 512, 4096], P('ep', 'tp', 'fsdp')
Inputs may be any that keep to these rules, and one draw needn't show every extreme that they name: Each row of routes names 2 different experts. In each token group of 128 consecutive rows no expert is named by more than 128 rows, a bound that some block reaches.
All inputs are finite; a program needn't handle non-finite values.
Results may differ from a plain program's by a relative error of at most 0.015.
Values may be sent and summed in bfloat16 or wider, within the bound.
A program may use at most 128 MiB of HBM per device.

v0:
```python
import jax
import jax.numpy as jnp
from jax import lax
from jax.sharding import PartitionSpec as P


def summed_rows(product, width, axis):
    whole = product(jnp.int32(0), width * lax.axis_size(axis)).astype(jnp.bfloat16)
    return lax.psum_scatter(whole, axis, scatter_dimension=0, tiled=True).astype(jnp.float32)


def slot_places(routes, experts, capacity):
    flat_routes = routes.reshape(-1)
    onehot = (flat_routes[:, None] == jnp.arange(experts, dtype=jnp.int32)[None, :]).astype(
        jnp.int32
    )
    earlier = (jnp.cumsum(onehot, axis=0) - onehot).astype(jnp.int32)
    position = jnp.sum(earlier * onehot, axis=1).astype(jnp.int32)
    return (flat_routes * capacity + position).astype(jnp.int32)


def weighted_rows(grad_rows, gate_probs):
    scaled = gate_probs[:, :, None] * grad_rows.astype(jnp.float32)[:, None, :]
    return scaled.astype(jnp.bfloat16).reshape(-1, grad_rows.shape[1])


def fill_slots(values, slot_index, total_slots):
    row_total = values.shape[0]
    source = jnp.full((total_slots,), row_total, jnp.int32)
    source = source.at[slot_index].set(jnp.arange(row_total, dtype=jnp.int32))
    padded = jnp.concatenate([values, jnp.zeros((1, values.shape[1]), values.dtype)], axis=0)
    return jnp.take(padded, source, axis=0)


def combine(returned, slot_index, tokens, per_token):
    picked = jnp.take(returned, slot_index, axis=0).astype(jnp.float32)
    return jnp.sum(picked.reshape(tokens, per_token, -1), axis=1).astype(jnp.bfloat16)


def transpose_dot(left, right):
    return lax.dot_general(
        left, right, (((0,), (0,)), ((), ())), preferred_element_type=jnp.float32
    )


def contract_last(left, right):
    return lax.dot_general(
        left, right, (((1,), (1,)), ((), ())), preferred_element_type=jnp.float32
    )


def body(out_grad, routes, chosen_logits, routed_inputs, w_gate, w_up, w_down):
    experts = lax.axis_size("ep")
    tp_count = lax.axis_size("tp")
    tokens, model_width = out_grad.shape
    per_token = routes.shape[1]
    capacity = routed_inputs.shape[3]
    gate_probs = jax.nn.softmax(chosen_logits, axis=-1)
    slot_index = slot_places(routes, experts, capacity)
    inputs = routed_inputs.reshape(-1, model_width)
    outgoing = fill_slots(weighted_rows(out_grad, gate_probs), slot_index, experts * capacity)
    arrived = lax.all_to_all(
        outgoing.reshape(experts, capacity, model_width),
        "ep",
        split_axis=0,
        concat_axis=0,
        tiled=True,
    )
    scaled = arrived.reshape(-1, model_width)
    gate_full, up_full, down_full = (
        lax.all_gather(w_gate, "fsdp", axis=1, tiled=True),
        lax.all_gather(w_up, "fsdp", axis=1, tiled=True),
        lax.all_gather(w_down, "fsdp", axis=2, tiled=True),
    )
    gate_full = gate_full[0]
    up_full = up_full[0]
    down_full = down_full[0]
    gate_act = jnp.dot(inputs, gate_full, preferred_element_type=jnp.float32)
    up_act = jnp.dot(inputs, up_full, preferred_element_type=jnp.float32)
    sigmoid_gate = jax.nn.sigmoid(gate_act)
    silu_gate = gate_act * sigmoid_gate
    hidden = (silu_gate * up_act).astype(jnp.bfloat16)
    hidden_grad = contract_last(scaled, down_full)
    products = jnp.sum(hidden_grad * hidden.astype(jnp.float32), axis=1)
    up_grad = (hidden_grad * silu_gate).astype(jnp.bfloat16)
    gate_grad = (
        hidden_grad * up_act * sigmoid_gate * (1.0 + gate_act * (1.0 - sigmoid_gate))
    ).astype(jnp.bfloat16)
    slot_part = contract_last(gate_grad, gate_full) + contract_last(up_grad, up_full)
    pair_grads = jnp.concatenate([gate_grad, up_grad], axis=1)

    def grad_term(first_row, row_count):
        input_cols = lax.dynamic_slice_in_dim(inputs, first_row, row_count, 1)
        scaled_cols = lax.dynamic_slice_in_dim(scaled, first_row, row_count, 1)
        gate_up_part = transpose_dot(input_cols, pair_grads)
        down_part = transpose_dot(scaled_cols, hidden)
        return jnp.concatenate([gate_up_part, down_part], axis=1)

    grad_rows = summed_rows(grad_term, model_width // lax.axis_size("fsdp"), "fsdp")
    hidden_units = hidden.shape[1]
    grad_gate = grad_rows[:, :hidden_units][None]
    grad_up = grad_rows[:, hidden_units : 2 * hidden_units][None]
    grad_down = grad_rows[:, 2 * hidden_units :].T[None]
    narrow = model_width // tp_count
    column_sum = lax.psum_scatter(
        slot_part.astype(jnp.bfloat16), "tp", scatter_dimension=1, tiled=True
    ).astype(jnp.float32)
    product_sum = lax.psum(products.astype(jnp.bfloat16), "tp").astype(jnp.float32)
    leaving = (
        column_sum.astype(jnp.bfloat16).reshape(experts, capacity, narrow),
        product_sum.astype(jnp.bfloat16).reshape(experts, capacity),
    )
    back_rows, back_products = (
        lax.all_to_all(leaving[0], "ep", split_axis=0, concat_axis=0, tiled=True),
        lax.all_to_all(leaving[1], "ep", split_axis=0, concat_axis=0, tiled=True),
    )
    combined = combine(back_rows.reshape(-1, narrow), slot_index, tokens, per_token)
    input_grad = lax.all_gather(combined, "tp", axis=1, tiled=True)
    chosen = (
        jnp.take(back_products.reshape(-1), slot_index)
        .astype(jnp.float32)
        .reshape(tokens, per_token)
    )
    logit_grad = chosen - gate_probs * jnp.sum(chosen, axis=1, keepdims=True)
    return (input_grad, logit_grad, grad_gate, grad_up, grad_down)


def solution(mesh):
    in_specs = (
        P(("ep", "fsdp"), None),
        P(("ep", "fsdp"), None),
        P(("ep", "fsdp"), None),
        P("ep", None, "fsdp", None, None),
        P("ep", "fsdp", "tp"),
        P("ep", "fsdp", "tp"),
        P("ep", "tp", "fsdp"),
    )
    out_specs = (
        P(("ep", "fsdp"), None),
        P(("ep", "fsdp"), None),
        P("ep", "fsdp", "tp"),
        P("ep", "fsdp", "tp"),
        P("ep", "tp", "fsdp"),
    )
    return jax.shard_map(body, mesh=mesh, in_specs=in_specs, out_specs=out_specs, check_vma=False)
```

profile of v0, /device:TPU:0, one launch (start us, length us, event | category | flops | bytes accessed | tf_op | source)
XLA Modules:
  0.0 295.3 jit_solution(5243169975518760738)
XLA Ops:
  12.3 1.4 scatter_custom_fusion
  16.1 5.3 %mul.79 = f32[128,2,4096]{2,1,0:T(2,128)} broadcast(bf16[128,4096]{1,0:T(8,128)(2,1)} %param.7), dimensions={0,2} | broadcast | bytes 5242880 | tf_op jit(solution)/shard_map/mul | solution.py:23
  21.4 6.1 %mul.80 = f32[256,4096]{1,0:T(8,128)} reshape(f32[128,2,4096]{2,1,0:T(2,128)} %mul.79) | data formatting | bytes 8388608 | tf_op jit(solution)/shard_map/mul | solution.py:23
  27.4 2.7 multiply_convert_fusion
  30.4 4.4 %gather_fusion = bf16[512,4096]{1,0:T(8,128)(2,1)} fusion(bf16[257,4096]{1,0:T(8,128)(2,1)S(1)} %concatenate.10, s32[1024]{0:T(1024)S(1)} %pad_clamp_fusion.1), kind=kCustom, calls=%fused_computation | custom fusion | bytes 8390656 | tf_op jit(solution)/shard_map/jit(_take)/gather | solution.py:32
  34.7 4.6 %broadcast_select_fusion = bf16[4,128,4096]{2,1,0:T(8,128)(2,1)} fusion(bf16[4,128,4096]{2,1,0:T(8,128)(2,1)} %bitcast.67, pred[4,128]{1,0:T(4,128)(4,1)S(1)} %and_bitcast_fusion), kind=kLoop, calls=%fused_computation.10 | loop fusion | flops 2097152 | bytes 8389120 | tf_op jit(solution)/shard_map/jit(_take)/select_n | solution.py:32
  39.3 6.4 %all-to-all-start = ((bf16[4,128,4096]{2,1,0:T(8,128)(2,1)}), bf16[4,128,4096]{2,1,0:T(8,128)(2,1)}, u32[]{:S(2)}, u32[]{:S(2)}) async-start(bf16[4,128,4096]{2,1,0:T(8,128)(2,1)} %broadcast_select_fusion), calls=%async_computation | async-start | bytes 8388608 | tf_op jit(solution)/shard_map/all_to_all | solution.py:62
  46.7 4.2 %fusion.3 = f32[512,256]{0,1:T(8,128)S(1)} fusion(bf16[512,4096]{1,0:T(8,128)(2,1)} %bitcast.74, bf16[1,4096,256]{2,1,0:T(8,128)(2,1)} %all-gather.9.cloned.1.call-done), kind=kOutput, calls=%fused_computation.13 | convolution fusion | flops 1073741824 | bytes 6815744 | tf_op jit(solution)/shard_map/dot_general | solution.py:78
  50.9 8.1 %all-gather.7.cloned.1.call-done = bf16[1,4096,256]{2,1,0:T(8,128)(2,1)} async-done(((bf16[1,1024,256]{2,1,0:T(8,128)(2,1)}), bf16[1,4096,256]{2,1,0:T(8,128)(2,1)}) %all-gather.7.cloned.1.call-update) | async-done | bytes 2097168 | tf_op jit(solution)/shard_map/all_gather | solution.py:72
  59.0 4.2 %fusion.6 = f32[512,256]{0,1:T(8,128)S(1)} fusion(bf16[512,4096]{1,0:T(8,128)(2,1)} %bitcast.75, bf16[1,4096,256]{2,1,0:T(8,128)(2,1)} %all-gather.7.cloned.1.call-done), kind=kOutput, calls=%fused_computation.16 | convolution fusion | flops 1073741824 | bytes 6815744 | tf_op jit(solution)/shard_map/dot_general | solution.py:79
  63.2 20.0 %all-gather.5.cloned.1.call-done = bf16[1,256,4096]{2,1,0:T(8,128)(2,1)} async-done(((bf16[1,256,1024]{2,1,0:T(8,128)(2,1)}), bf16[1,256,4096]{2,1,0:T(8,128)(2,1)}) %all-gather.5.cloned.1.call-update) | async-done | bytes 2097168 | tf_op jit(solution)/shard_map/all_gather | solution.py:73
  83.2 56.0 %all-to-all-done = bf16[4,128,4096]{2,1,0:T(8,128)(2,1)} async-done(((bf16[4,128,4096]{2,1,0:T(8,128)(2,1)}), bf16[4,128,4096]{2,1,0:T(8,128)(2,1)}, u32[]{:S(2)}, u32[]{:S(2)}) %all-to-all-start) | async-done | bytes 4194336 | tf_op jit(solution)/shard_map/all_to_all | solution.py:62
  139.2 4.5 %multiply_reduce_fusion = (bf16[512]{0:T(512)(128)(2,1)S(1)}, bf16[512,256]{0,1:T(8,128)(2,1)S(1)}, bf16[512,256]{0,1:T(8,128)(2,1)S(1)}, bf16[512,256]{0,1:T(8,128)(2,1)S(1)}) fusion(f32[512,256]{0,1:T(8,128)S(1)} %fusion.6, f32[512,256]{0,1:T(8,128)S(1)} %fusion.3, bf16[512,4096]{1,0:T(8,128)(2,1)} %bitcast.6, ...), kind=kOutput, calls=%fused_computation.28 | convolution fusion | flops 1076100608 | bytes 8127488 | tf_op jit(solution)/shard_map/dot_general | solution.py:47
  143.7 1.3 fusion.1
  145.3 3.4 %add_convert_fusion = bf16[512,4096]{1,0:T(8,128)(2,1)} fusion(f32[512,4096]{1,0:T(8,128)S(1)} %fusion.1, bf16[512,256]{0,1:T(8,128)(2,1)S(1)} %get-tuple-element.33, bf16[1,4096,256]{2,1,0:T(8,128)(2,1)S(1)} %copy-done), kind=kOutput, calls=%fused_computation.4 | convolution fusion | flops 1077936128 | bytes 14942208 | tf_op jit(solution)/shard_map/dot_general | solution.py:47
  148.8 3.7 %convolution_convert_fusion.1 = bf16[4096,256]{0,1:T(8,128)(2,1)S(1)} fusion(bf16[512,256]{0,1:T(8,128)(2,1)S(1)} %get-tuple-element.28, bf16[512,4096]{1,0:T(8,128)(2,1)} %bitcast.6), kind=kOutput, calls=%fused_computation.8 | convolution fusion | flops 1074790400 | bytes 6553600 | tf_op jit(solution)/shard_map/dot_general | solution.py:41
  152.5 2.4 fusion
  154.9 3.4 %pad_maximum_fusion = bf16[4096,768]{0,1:T(8,128)(2,1)} fusion(bf16[4096,256]{0,1:T(8,128)(2,1)S(1)} %convolution_convert_fusion.1, bf16[4096,512]{0,1:T(8,128)(2,1)S(1)} %fusion), kind=kLoop, calls=%fused_computation.5 | loop fusion | flops 12582912 | bytes 12582912 | tf_op jit(solution)/shard_map/concatenate | solution.py:97
  158.4 5.1 %psum.7 = bf16[4,1,128]{2,0,1:T(4,128)(2,1)S(1)} all-reduce(bf16[4,1,128]{2,0,1:T(4,128)(2,1)S(1)} %bitcast.73), channel_id=1, replica_groups=mesh['ep'=4,'fsdp'=4,'tp'=2] {'tp'}, use_global_device_ids=true, to_apply=%region_9.10 | all-reduce | flops 512 | bytes 2048 | tf_op jit(solution)/shard_map/psum | solution.py:108
  163.5 8.0 %all_to_all.19 = bf16[4,1,128]{2,1,0:T(2,128)(2,1)S(1)} all-to-all(bf16[4,1,128]{2,1,0:T(2,128)(2,1)S(1)} %copy.46), channel_id=1, replica_groups=mesh['ep'=4,'fsdp'=4,'tp'=2] {'ep'}, dimensions={0} | all-to-all | bytes 2048 | tf_op jit(solution)/shard_map/all_to_all | solution.py:115
  171.5 31.0 %reduce-scatter.3.cloned.1.call-done = bf16[512,2048]{1,0:T(8,128)(2,1)} async-done(((bf16[512,4096]{1,0:T(8,128)(2,1)}), bf16[512,2048]{1,0:T(8,128)(2,1)}) %reduce-scatter.3.cloned.1.call-update) | async-done | bytes 2097168 | tf_op jit(solution)/shard_map/reduce_scatter | solution.py:105
  202.5 4.6 %all-to-all-start.1 = ((bf16[4,128,2048]{2,1,0:T(8,128)(2,1)}), bf16[4,128,2048]{2,1,0:T(8,128)(2,1)S(1)}, u32[]{:S(2)}, u32[]{:S(2)}) async-start(bf16[4,128,2048]{2,1,0:T(8,128)(2,1)} %bitcast.68), calls=%async_computation.2 | async-start | bytes 4194304 | tf_op jit(solution)/shard_map/all_to_all | solution.py:114
  207.4 1.9 gather_fusion.2
  209.7 45.4 %all-to-all-done.1 = bf16[4,128,2048]{2,1,0:T(8,128)(2,1)S(1)} async-done(((bf16[4,128,2048]{2,1,0:T(8,128)(2,1)}), bf16[4,128,2048]{2,1,0:T(8,128)(2,1)S(1)}, u32[]{:S(2)}, u32[]{:S(2)}) %all-to-all-start.1) | async-done | bytes 2097184 | tf_op jit(solution)/shard_map/all_to_all | solution.py:114
  255.1 1.4 gather_fusion.1
  257.2 3.2 %fusion.10 = bf16[128,2048]{1,0:T(8,128)(2,1)} fusion(bf16[128,2,2048]{2,1,0:T(2,128)(2,1)S(1)} %gather.21, pred[128,2]{1,0:T(8,128)(4,1)S(1)} %copy.43), kind=kLoop, calls=%fused_computation.21 | loop fusion | flops 786432 | bytes 1573120 | tf_op jit(solution)/shard_map/reduce_sum | solution.py:37
  261.0 1.8 reduce-scatter.5.cloned.1.call-done
  262.8 1.8 convert_element_type.58
  265.8 1.3 copy.48
  267.1 1.3 copy.49
  268.4 17.7 %all-gather.11.cloned.1.call-done = bf16[128,4096]{1,0:T(8,128)(2,1)} async-done(((bf16[128,2048]{1,0:T(8,128)(2,1)}), bf16[128,4096]{1,0:T(8,128)(2,1)}) %all-gather.11.cloned.1.call-update) | async-done | bytes 1048592 | tf_op jit(solution)/shard_map/all_gather | solution.py:118
  286.1 2.3 copy.53
  (61 shorter events, 12.2 us)
Async XLA Ops:
  7.2 39.5 %all-gather.9.cloned.1.call-start = ((), (), s32[]{:S(2)}) async-start(), calls=%async_computation.7 | async-start | bytes 2621440 | tf_op jit(solution)/shard_map/all_gather | solution.py:71
  7.9 51.1 %all-gather.7.cloned.1.call-start = ((), (), s32[]{:S(2)}) async-start(), calls=%async_computation.6 | async-start | bytes 2621440 | tf_op jit(solution)/shard_map/all_gather | solution.py:72
  39.3 99.9 %all-to-all-start = ((bf16[4,128,4096]{2,1,0:T(8,128)(2,1)}), bf16[4,128,4096]{2,1,0:T(8,128)(2,1)}, u32[]{:S(2)}, u32[]{:S(2)}) async-start(bf16[4,128,4096]{2,1,0:T(8,128)(2,1)} %broadcast_select_fusion), calls=%async_computation | async-start | bytes 8388608 | tf_op jit(solution)/shard_map/all_to_all | solution.py:62
  45.7 37.5 %all-gather.5.cloned.1.call-start = ((), (), s32[]{:S(2)}) async-start(), calls=%async_computation.5 | async-start | bytes 2621440 | tf_op jit(solution)/shard_map/all_gather | solution.py:73
  46.4 156.1 %reduce-scatter.3.cloned.1.call-start = ((), (), s32[]{:S(2)}) async-start(), calls=%async_computation.8 | async-start | bytes 6291456 | tf_op jit(solution)/shard_map/reduce_scatter | solution.py:105
  139.2 4.5 %copy-start.1 = (bf16[1,4096,256]{2,1,0:T(8,128)(2,1)S(1)}, bf16[1,4096,256]{2,1,0:T(8,128)(2,1)}, u32[]{:S(2)}) copy-start(bf16[1,4096,256]{2,1,0:T(8,128)(2,1)} %all-gather.9.cloned.1.call-done) | copy-start | bytes 6291460
  143.7 1.6 copy-start
  148.8 114.1 %reduce-scatter.5.cloned.1.call-start = ((), (), s32[]{:S(2)}) async-start(), calls=%async_computation.10 | async-start | bytes 7864320 | tf_op jit(solution)/shard_map/reduce_scatter | solution.py:9
  148.8 3.7 %copy-start.4 = (bf16[1,4,1,128,4096]{4,3,2,1,0:T(8,128)(2,1)S(1)}, bf16[1,4,1,128,4096]{4,3,2,1,0:T(8,128)(2,1)}, u32[]{:S(2)}) copy-start(bf16[1,4,1,128,4096]{4,3,2,1,0:T(8,128)(2,1)} %param.10) | copy-start | bytes 12582916
  158.3 51.2 %copy-start.3 = (s32[128,2]{0,1:T(2,128)S(1)}, s32[128,2]{0,1:T(2,128)}, u32[]{:S(2)}) copy-start(s32[128,2]{0,1:T(2,128)} %param.8) | copy-start | bytes 3076
  202.5 52.6 %all-to-all-start.1 = ((bf16[4,128,2048]{2,1,0:T(8,128)(2,1)}), bf16[4,128,2048]{2,1,0:T(8,128)(2,1)S(1)}, u32[]{:S(2)}, u32[]{:S(2)}) async-start(bf16[4,128,2048]{2,1,0:T(8,128)(2,1)} %bitcast.68), calls=%async_computation.2 | async-start | bytes 4194304 | tf_op jit(solution)/shard_map/all_to_all | solution.py:114
  207.1 79.0 %all-gather.11.cloned.1.call-start = ((), (), s32[]{:S(2)}) async-start(), calls=%async_computation.9 | async-start | bytes 1572864 | tf_op jit(solution)/shard_map/all_gather | solution.py:118
  256.5 3.9 %copy-start.2 = (f32[128,2]{0,1:T(2,128)S(1)}, f32[128,2]{0,1:T(2,128)}, u32[]{:S(2)}) copy-start(f32[128,2]{0,1:T(2,128)} %param.9) | copy-start | bytes 3076
Sparse Core Ops, SparseCore 0:
  9.5 25.2 all-gather.8
  36.4 22.5 all-gather.6
  60.6 22.5 all-gather.4
  148.9 53.5 reduce-scatter.2
  204.9 57.8 reduce-scatter.4
  264.8 21.2 all-gather.10
where the time goes:
time: 296 us; the launch traced here: 295 us
  waiting for transfers between devices  182 us (61%)
  local copies, waits for them, and re-layouts  30.2 us (10%)
  matrix products  23.6 us (8%)
  other arithmetic  20.4 us (7%)
  between operations  14.3 us (5%)
  blocking collectives  13.1 us (4%)
  starting transfers between devices  11.3 us (4%)
    all_to_all x1, waiting for transfers between devices, body(): lax.all_to_all(outgoing.reshape(experts, capacity, model_width), 'ep', sp...  56 us
    all_to_all x1, waiting for transfers between devices, body(): lax.all_to_all(leaving[0], 'ep', split_axis=0, concat_axis=0, tiled=True)  45.4 us
    reduce_scatter x1, waiting for transfers between devices, body(): lax.psum_scatter(slot_part.astype(jnp.bfloat16), 'tp', scatter_dimension=...  31 us
    all_gather x1, waiting for transfers between devices, body(): lax.all_gather(w_down, 'fsdp', axis=2, tiled=True)  20 us
    all_gather x1, waiting for transfers between devices, body(): input_grad = lax.all_gather(combined, 'tp', axis=1, tiled=True)  17.7 us
    mul x3, local copies, waits for them, and re-layouts, weighted_rows(): scaled = gate_probs[:, :, None] * grad_rows.astype(jnp.float32)[:, None, :]  11.5 us
    dot_general x3, matrix products, contract_last(): lax.dot_general(left, right, (((1,), (1,)), ((), ())), preferred_element_...  9.23 us
    all_gather x1, waiting for transfers between devices, body(): lax.all_gather(w_up, 'fsdp', axis=1, tiled=True)  8.14 us
  transfers between devices with their start and end apart: 8, of which 7 were waited for; matrix products, arithmetic and copies ran while one was open for 21% of the time, Pallas kernels for 0%

commit v1 on v0

--- a/solution.py
+++ b/solution.py
@@ -1,7 +1,18 @@
+import functools
 import jax
 import jax.numpy as jnp
 from jax import lax
 from jax.sharding import PartitionSpec as P
+
+
+def apply_sources_all(raw, axis_id):
+    aux = jnp.stack(lax.axis_size(axis_id) * [raw], 0)
+    raw_out = lax.all_to_all(aux, axis_id, 0, 0)
+    after = jnp.concatenate(raw_out, 2)
+    return after
+
+
+remake_the_turns = functools.partial(apply_sources_all, axis_id="fsdp")
 
 
 def summed_rows(product, width, axis):
@@ -70,7 +81,7 @@
     gate_full, up_full, down_full = (
         lax.all_gather(w_gate, "fsdp", axis=1, tiled=True),
         lax.all_gather(w_up, "fsdp", axis=1, tiled=True),
-        lax.all_gather(w_down, "fsdp", axis=2, tiled=True),
+        remake_the_turns(w_down),
     )
     gate_full = gate_full[0]
     up_full = up_full[0]

time: 296 us -> 307 us (1.037)
  waiting for transfers between devices: 182 us -> 192 us
  starting transfers between devices: 11.3 us -> 15.1 us
    all_gather x1 -> x0, waiting for transfers between devices: 20 us -> none  [body(): lax.all_gather(w_down, 'fsdp', axis=2, tiled=True)]
    all_gather x1, waiting for transfers between devices: 8.14 us -> 20.3 us  [body(): lax.all_gather(w_up, 'fsdp', axis=1, tiled=True)]
    all_to_all x0 -> x1, waiting for transfers between devices: none -> 11.5 us  [apply_sources_all(): raw_out = lax.all_to_all(aux, axis_id, 0, 0)]
    all_to_all x1, waiting for transfers between devices: 56 us -> 63.5 us  [body(): lax.all_to_all(outgoing.reshape(experts, capacity, model_width), 'ep', sp...]
    all_to_all x0 -> x1, starting transfers between devices: none -> 4.48 us  [apply_sources_all(): raw_out = lax.all_to_all(aux, axis_id, 0, 0)]
  transfers between devices with their start and end apart: 8 -> 8, of which waited for: 7 -> 7; matrix products, arithmetic and copies ran while one was open for 21% -> 20% of each run, Pallas kernels for 0% -> 0%
where the time goes in v1:
time: 307 us
  waiting for transfers between devices  192 us (63%)
  local copies, waits for them, and re-layouts  31.1 us (10%)
  matrix products  23.6 us (8%)
  other arithmetic  17.7 us (6%)
  starting transfers between devices  15.1 us (5%)
  between operations  14 us (5%)
  blocking collectives  13.2 us (4%)
    all_to_all x1, waiting for transfers between devices, body(): lax.all_to_all(outgoing.reshape(experts, capacity, model_width), 'ep', sp...  63.5 us
    all_to_all x1, waiting for transfers between devices, body(): lax.all_to_all(leaving[0], 'ep', split_axis=0, concat_axis=0, tiled=True)  45.4 us
    reduce_scatter x1, waiting for transfers between devices, body(): lax.psum_scatter(slot_part.astype(jnp.bfloat16), 'tp', scatter_dimension=...  30.3 us
    all_gather x1, waiting for transfers between devices, body(): lax.all_gather(w_up, 'fsdp', axis=1, tiled=True)  20.3 us
    all_gather x1, waiting for transfers between devices, body(): input_grad = lax.all_gather(combined, 'tp', axis=1, tiled=True)  17.7 us
    all_to_all x1, waiting for transfers between devices, apply_sources_all(): raw_out = lax.all_to_all(aux, axis_id, 0, 0)  11.5 us
    mul x3, local copies, waits for them, and re-layouts, weighted_rows(): scaled = gate_probs[:, :, None] * grad_rows.astype(jnp.float32)[:, None, :]  10.2 us
    dot_general x3, matrix products, contract_last(): lax.dot_general(left, right, (((1,), (1,)), ((), ())), preferred_element_...  9.24 us
  transfers between devices with their start and end apart: 8, of which 7 were waited for; matrix products, arithmetic and copies ran while one was open for 20% of the time, Pallas kernels for 0%

profile of v1, /device:TPU:0, one launch (start us, length us, event | category | flops | bytes accessed | tf_op | source)
XLA Modules:
  0.0 306.7 jit_solution(9915884389368124648)
XLA Ops:
  7.9 1.3 copy.49
  9.3 1.5 stack.2
  10.8 4.5 %all-to-all-start.1 = ((bf16[4,1,256,1024]{2,3,1,0:T(8,128)(2,1)}), bf16[4,1,256,1024]{2,3,1,0:T(8,128)(2,1)}, u32[]{:S(2)}, u32[]{:S(2)}) async-start(bf16[4,1,256,1024]{2,3,1,0:T(8,128)(2,1)} %stack.2), calls=%async_computation.1 | async-start | bytes 4194304 | tf_op jit(solution)/shard_map/all_to_all | solution.py:10
  17.9 4.0 %mul.79 = f32[128,2,4096]{2,1,0:T(2,128)} broadcast(bf16[128,4096]{1,0:T(8,128)(2,1)S(1)} %copy-done.2), dimensions={0,2} | broadcast | bytes 5242880 | tf_op jit(solution)/shard_map/mul | solution.py:34
  21.9 6.0 %mul.80 = f32[256,4096]{1,0:T(8,128)} reshape(f32[128,2,4096]{2,1,0:T(2,128)} %mul.79) | data formatting | bytes 8388608 | tf_op jit(solution)/shard_map/mul | solution.py:34
  28.0 2.7 multiply_convert_fusion
  30.9 1.4 scatter_custom_fusion
  32.4 4.4 %gather_fusion = bf16[512,4096]{1,0:T(8,128)(2,1)} fusion(bf16[257,4096]{1,0:T(8,128)(2,1)S(1)} %concatenate.10, s32[1024]{0:T(1024)S(1)} %pad_clamp_fusion.1), kind=kCustom, calls=%fused_computation | custom fusion | bytes 8390656 | tf_op jit(solution)/shard_map/jit(_take)/gather | solution.py:43
  36.7 4.6 %broadcast_select_fusion = bf16[4,128,4096]{2,1,0:T(8,128)(2,1)} fusion(bf16[4,128,4096]{2,1,0:T(8,128)(2,1)} %bitcast.69, pred[4,128]{1,0:T(4,128)(4,1)S(1)} %and_bitcast_fusion), kind=kLoop, calls=%fused_computation.10 | loop fusion | flops 2097152 | bytes 8389120 | tf_op jit(solution)/shard_map/jit(_take)/select_n | solution.py:43
  41.3 11.5 %all-to-all-done.1 = bf16[4,1,256,1024]{2,3,1,0:T(8,128)(2,1)} async-done(((bf16[4,1,256,1024]{2,3,1,0:T(8,128)(2,1)}), bf16[4,1,256,1024]{2,3,1,0:T(8,128)(2,1)}, u32[]{:S(2)}, u32[]{:S(2)}) %all-to-all-start.1) | async-done | bytes 2097184 | tf_op jit(solution)/shard_map/all_to_all | solution.py:10
  52.9 5.7 %all-to-all-start = ((bf16[4,128,4096]{2,1,0:T(8,128)(2,1)}), bf16[4,128,4096]{2,1,0:T(8,128)(2,1)}, u32[]{:S(2)}, u32[]{:S(2)}) async-start(bf16[4,128,4096]{2,1,0:T(8,128)(2,1)} %broadcast_select_fusion), calls=%async_computation | async-start | bytes 8388608 | tf_op jit(solution)/shard_map/all_to_all | solution.py:73
  59.5 4.2 %fusion.3 = f32[512,256]{0,1:T(8,128)S(1)} fusion(bf16[512,4096]{1,0:T(8,128)(2,1)} %bitcast.77, bf16[1,4096,256]{2,1,0:T(8,128)(2,1)} %all-gather.6.cloned.1.call-done), kind=kOutput, calls=%fused_computation.13 | convolution fusion | flops 1073741824 | bytes 6815744 | tf_op jit(solution)/shard_map/dot_general | solution.py:89
  63.7 20.3 %all-gather.4.cloned.1.call-done = bf16[1,4096,256]{2,1,0:T(8,128)(2,1)} async-done(((bf16[1,1024,256]{2,1,0:T(8,128)(2,1)}), bf16[1,4096,256]{2,1,0:T(8,128)(2,1)}) %all-gather.4.cloned.1.call-update) | async-done | bytes 2097168 | tf_op jit(solution)/shard_map/all_gather | solution.py:83
  84.1 4.2 %fusion.6 = f32[512,256]{0,1:T(8,128)S(1)} fusion(bf16[512,4096]{1,0:T(8,128)(2,1)} %bitcast.78, bf16[1,4096,256]{2,1,0:T(8,128)(2,1)} %all-gather.4.cloned.1.call-done), kind=kOutput, calls=%fused_computation.16 | convolution fusion | flops 1073741824 | bytes 6815744 | tf_op jit(solution)/shard_map/dot_general | solution.py:90
  88.2 63.5 %all-to-all-done = bf16[4,128,4096]{2,1,0:T(8,128)(2,1)} async-done(((bf16[4,128,4096]{2,1,0:T(8,128)(2,1)}), bf16[4,128,4096]{2,1,0:T(8,128)(2,1)}, u32[]{:S(2)}, u32[]{:S(2)}) %all-to-all-start) | async-done | bytes 4194336 | tf_op jit(solution)/shard_map/all_to_all | solution.py:73
  151.7 4.5 %multiply_reduce_fusion = (bf16[512]{0:T(512)(128)(2,1)S(1)}, bf16[512,256]{0,1:T(8,128)(2,1)S(1)}, bf16[512,256]{0,1:T(8,128)(2,1)S(1)}, bf16[512,256]{0,1:T(8,128)(2,1)S(1)}) fusion(f32[512,256]{0,1:T(8,128)S(1)} %fusion.6, f32[512,256]{0,1:T(8,128)S(1)} %fusion.3, bf16[512,4096]{1,0:T(8,128)(2,1)} %bitcast.6, bf16[256,4096]{0,1:T(8,128)(2,1)} %bitcast.10), kind=kOutput, calls=%fused_computation.26 | convolution fusion | flops 1076100608 | bytes 8127488 | tf_op jit(solution)/shard_map/dot_general | solution.py:58
  157.8 3.4 %add_convert_fusion = bf16[512,4096]{1,0:T(8,128)(2,1)} fusion(f32[512,4096]{1,0:T(8,128)S(1)} %fusion.1, bf16[512,256]{0,1:T(8,128)(2,1)S(1)} %get-tuple-element.33, bf16[1,4096,256]{2,1,0:T(8,128)(2,1)S(1)} %copy-done), kind=kOutput, calls=%fused_computation.4 | convolution fusion | flops 1077936128 | bytes 14942208 | tf_op jit(solution)/shard_map/dot_general | solution.py:58
  161.3 3.6 %convolution_convert_fusion.1 = bf16[4096,256]{0,1:T(8,128)(2,1)S(1)} fusion(bf16[512,256]{0,1:T(8,128)(2,1)S(1)} %get-tuple-element.28, bf16[512,4096]{1,0:T(8,128)(2,1)} %bitcast.6), kind=kOutput, calls=%fused_computation.8 | convolution fusion | flops 1074790400 | bytes 6553600 | tf_op jit(solution)/shard_map/dot_general | solution.py:52
  164.9 2.4 fusion
  167.3 3.4 %pad_maximum_fusion = bf16[4096,768]{0,1:T(8,128)(2,1)} fusion(bf16[4096,256]{0,1:T(8,128)(2,1)S(1)} %convolution_convert_fusion.1, bf16[4096,512]{0,1:T(8,128)(2,1)S(1)} %fusion), kind=kLoop, calls=%fused_computation.5 | loop fusion | flops 12582912 | bytes 12582912 | tf_op jit(solution)/shard_map/concatenate | solution.py:108
  170.8 5.1 %psum.7 = bf16[4,1,128]{2,0,1:T(4,128)(2,1)S(1)} all-reduce(bf16[4,1,128]{2,0,1:T(4,128)(2,1)S(1)} %bitcast.76), channel_id=1, replica_groups=mesh['ep'=4,'fsdp'=4,'tp'=2] {'tp'}, use_global_device_ids=true, to_apply=%region_9.10 | all-reduce | flops 512 | bytes 2048 | tf_op jit(solution)/shard_map/psum | solution.py:119
  175.9 8.0 %all_to_all.24 = bf16[4,1,128]{2,1,0:T(2,128)(2,1)S(1)} all-to-all(bf16[4,1,128]{2,1,0:T(2,128)(2,1)S(1)} %copy.51), channel_id=1, replica_groups=mesh['ep'=4,'fsdp'=4,'tp'=2] {'ep'}, dimensions={0} | all-to-all | bytes 2048 | tf_op jit(solution)/shard_map/all_to_all | solution.py:126
  184.0 30.3 %reduce-scatter.3.cloned.1.call-done = bf16[512,2048]{1,0:T(8,128)(2,1)} async-done(((bf16[512,4096]{1,0:T(8,128)(2,1)}), bf16[512,2048]{1,0:T(8,128)(2,1)}) %reduce-scatter.3.cloned.1.call-update) | async-done | bytes 2097168 | tf_op jit(solution)/shard_map/reduce_scatter | solution.py:116
  214.3 4.6 %all-to-all-start.2 = ((bf16[4,128,2048]{2,1,0:T(8,128)(2,1)}), bf16[4,128,2048]{2,1,0:T(8,128)(2,1)S(1)}, u32[]{:S(2)}, u32[]{:S(2)}) async-start(bf16[4,128,2048]{2,1,0:T(8,128)(2,1)} %bitcast.70), calls=%async_computation.3 | async-start | bytes 4194304 | tf_op jit(solution)/shard_map/all_to_all | solution.py:125
  219.1 1.9 gather_fusion.2
  221.5 45.4 %all-to-all-done.2 = bf16[4,128,2048]{2,1,0:T(8,128)(2,1)S(1)} async-done(((bf16[4,128,2048]{2,1,0:T(8,128)(2,1)}), bf16[4,128,2048]{2,1,0:T(8,128)(2,1)S(1)}, u32[]{:S(2)}, u32[]{:S(2)}) %all-to-all-start.2) | async-done | bytes 2097184 | tf_op jit(solution)/shard_map/all_to_all | solution.py:125
  266.9 1.4 gather_fusion.1
  269.0 3.2 %fusion.8 = bf16[128,2048]{1,0:T(8,128)(2,1)} fusion(bf16[128,2,2048]{2,1,0:T(2,128)(2,1)S(1)} %gather.21, pred[128,2]{1,0:T(8,128)(4,1)S(1)} %copy.46), kind=kLoop, calls=%fused_computation.19 | loop fusion | flops 786432 | bytes 1573120 | tf_op jit(solution)/shard_map/reduce_sum | solution.py:48
  272.8 1.8 reduce-scatter.5.cloned.1.call-done
  274.6 1.8 convert_element_type.58
  280.2 17.7 %all-gather.8.cloned.1.call-done = bf16[128,4096]{1,0:T(8,128)(2,1)} async-done(((bf16[128,2048]{1,0:T(8,128)(2,1)}), bf16[128,4096]{1,0:T(8,128)(2,1)}) %all-gather.8.cloned.1.call-update) | async-done | bytes 1048592 | tf_op jit(solution)/shard_map/all_gather | solution.py:129
  297.9 2.3 copy.58
  (64 shorter events, 12.0 us)
Async XLA Ops:
  7.2 8.1 %copy-start.4 = (s32[128,2]{0,1:T(2,128)S(1)}, s32[128,2]{0,1:T(2,128)}, u32[]{:S(2)}) copy-start(s32[128,2]{0,1:T(2,128)} %param.8) | copy-start | bytes 3076
  7.2 52.4 %all-gather.6.cloned.1.call-start = ((), (), s32[]{:S(2)}) async-start(), calls=%async_computation.7 | async-start | bytes 2621440 | tf_op jit(solution)/shard_map/all_gather | solution.py:82
  7.9 9.6 %copy-start.3 = (f32[128,2]{0,1:T(2,128)S(1)}, f32[128,2]{0,1:T(2,128)}, u32[]{:S(2)}) copy-start(f32[128,2]{0,1:T(2,128)} %param.9) | copy-start | bytes 3076
  7.9 10.0 %copy-start.2 = (bf16[128,4096]{1,0:T(8,128)(2,1)S(1)}, bf16[128,4096]{1,0:T(8,128)(2,1)}, u32[]{:S(2)}) copy-start(bf16[128,4096]{1,0:T(8,128)(2,1)} %param.7) | copy-start | bytes 3145732
  10.8 42.1 %all-to-all-start.1 = ((bf16[4,1,256,1024]{2,3,1,0:T(8,128)(2,1)}), bf16[4,1,256,1024]{2,3,1,0:T(8,128)(2,1)}, u32[]{:S(2)}, u32[]{:S(2)}) async-start(bf16[4,1,256,1024]{2,3,1,0:T(8,128)(2,1)} %stack.2), calls=%async_computation.1 | async-start | bytes 4194304 | tf_op jit(solution)/shard_map/all_to_all | solution.py:10
  52.9 98.8 %all-to-all-start = ((bf16[4,128,4096]{2,1,0:T(8,128)(2,1)}), bf16[4,128,4096]{2,1,0:T(8,128)(2,1)}, u32[]{:S(2)}, u32[]{:S(2)}) async-start(bf16[4,128,4096]{2,1,0:T(8,128)(2,1)} %broadcast_select_fusion), calls=%async_computation | async-start | bytes 8388608 | tf_op jit(solution)/shard_map/all_to_all | solution.py:73
  58.6 25.5 %all-gather.4.cloned.1.call-start = ((), (), s32[]{:S(2)}) async-start(), calls=%async_computation.6 | async-start | bytes 2621440 | tf_op jit(solution)/shard_map/all_gather | solution.py:83
  59.3 155.0 %reduce-scatter.3.cloned.1.call-start = ((), (), s32[]{:S(2)}) async-start(), calls=%async_computation.8 | async-start | bytes 6291456 | tf_op jit(solution)/shard_map/reduce_scatter | solution.py:116
  151.7 4.5 %copy-start.1 = (bf16[1,4096,256]{2,1,0:T(8,128)(2,1)S(1)}, bf16[1,4096,256]{2,1,0:T(8,128)(2,1)}, u32[]{:S(2)}) copy-start(bf16[1,4096,256]{2,1,0:T(8,128)(2,1)} %all-gather.6.cloned.1.call-done) | copy-start | bytes 6291460
  156.2 1.6 copy-start
  161.2 113.3 %reduce-scatter.5.cloned.1.call-start = ((), (), s32[]{:S(2)}) async-start(), calls=%async_computation.10 | async-start | bytes 7864320 | tf_op jit(solution)/shard_map/reduce_scatter | solution.py:20
  161.3 3.6 %copy-start.5 = (bf16[1,4,1,128,4096]{4,3,2,1,0:T(8,128)(2,1)S(1)}, bf16[1,4,1,128,4096]{4,3,2,1,0:T(8,128)(2,1)}, u32[]{:S(2)}) copy-start(bf16[1,4,1,128,4096]{4,3,2,1,0:T(8,128)(2,1)} %param.10) | copy-start | bytes 12582916
  214.3 52.6 %all-to-all-start.2 = ((bf16[4,128,2048]{2,1,0:T(8,128)(2,1)}), bf16[4,128,2048]{2,1,0:T(8,128)(2,1)S(1)}, u32[]{:S(2)}, u32[]{:S(2)}) async-start(bf16[4,128,2048]{2,1,0:T(8,128)(2,1)} %bitcast.70), calls=%async_computation.3 | async-start | bytes 4194304 | tf_op jit(solution)/shard_map/all_to_all | solution.py:125
  218.9 79.0 %all-gather.8.cloned.1.call-start = ((), (), s32[]{:S(2)}) async-start(), calls=%async_computation.9 | async-start | bytes 1572864 | tf_op jit(solution)/shard_map/all_gather | solution.py:129
Sparse Core Ops, SparseCore 0:
  9.5 36.6 all-gather.5
  60.9 23.0 all-gather.3
  161.4 52.8 reduce-scatter.2
  216.7 57.8 reduce-scatter.4
  276.6 21.2 all-gather.7
